TPU v7x, 32 devices: a whole 2x2x4 slice. The times are simulated.
32 devices in a mesh: grp: 2 (over y), seq: 16 (over z, x, core).
Axes of the slice: x: 2, y: 2, z: 4, core: 2. Of those that a mesh axis runs over, the one named last changes fastest.
Arguments:
- history: bfloat16 [8192, 1024], P(('grp', 'seq')), parts along dimension 0, may hold values from -6 to 6
- candidates: bfloat16 [512, 1024], P(('grp', 'seq')), parts along dimension 0, may hold values from -6 to 6
- lengths: int32 [8], P('grp'), parts along dimension 0, may hold values from 1 to 2048, 4096 in all
- cand_user: int32 [512], P(('grp', 'seq')), parts along dimension 0, may hold values from 0 to 3
- w_in: bfloat16 [1, 1024, 4096], replicated, may hold values from -0.125 to 0.125
- w_out: bfloat16 [1, 1024, 1024], replicated, may hold values from -0.1875 to 0.1875
Outputs:
- history_out: bfloat16 [8192, 1024], P(('grp', 'seq')), parts along dimension 0
- cand_out: bfloat16 [512, 1024], P(('grp', 'seq')), parts along dimension 0
There are 2 independent parts, one for each index of `grp`. A program takes and returns all parts, laid end to end along the dimension named above; an argument that names none is the same for every part. Nothing has to cross between parts.
Inputs may be any that keep to these rules, and one draw needn't show every extreme that they name: Each user's history length is at least 1; the lengths sum to 4096, and one of them is exactly 2048.
All inputs are finite; a program needn't handle non-finite values.
Results may differ from a plain program's by a relative error of at most 0.0075.
Values may be sent and summed in bfloat16 or wider, within the bound.
A program may use at most 128 MiB of HBM per device.

v0:
```python
import jax
import jax.numpy as jnp
from jax import lax
from jax.sharding import PartitionSpec as P

HEADS = 8
WIN = 8
eps = 1e-06


def passed_along(value, axis, by):
    peers = lax.axis_size(axis)
    pairs = [(i, i + by) for i in range(peers) if 0 <= i + by < peers]
    return lax.ppermute(value, axis, pairs)


def layer_norm(rows):
    centred = rows - jnp.mean(rows, axis=-1, keepdims=True)
    return centred * lax.rsqrt(jnp.mean(centred * centred, axis=-1, keepdims=True) + eps)


def segment_of(positions, ends):
    return jnp.sum((positions[:, None] >= ends[None, :]).astype(jnp.int32), axis=1)


def per_device(history, candidates, lengths, cand_user, w_in, w_out):
    rows = history.shape[0]
    width = history.shape[1]
    heads = HEADS
    head_dim = width // heads
    scale = head_dim ** (-0.5)
    reach = (WIN - 1) * rows
    myself = lax.axis_index("seq")
    ends = jnp.cumsum(lengths)
    q_pos = myself * rows + jnp.arange(rows, dtype=jnp.int32)
    q_seg = segment_of(q_pos, ends)
    k_pos = myself * rows - (WIN - 1) * rows + jnp.arange(WIN * rows, dtype=jnp.int32)
    allowed = (k_pos[None, :] >= 0) & (k_pos[None, :] <= q_pos[:, None])
    allowed = allowed & (q_pos[:, None] - k_pos[None, :] < reach)
    allowed = allowed & (segment_of(k_pos, ends)[None, :] == q_seg[:, None])
    x_rows = history
    c_rows = candidates
    normed = layer_norm(x_rows.astype(jnp.float32)).astype(jnp.bfloat16)
    proj = jax.nn.silu(jnp.dot(normed, w_in[0], preferred_element_type=jnp.float32)).astype(
        jnp.bfloat16
    )
    u_all = proj[:, 0:width]
    v_all = proj[:, width : 2 * width]
    q_all = proj[:, 2 * width : 3 * width]
    k_all = proj[:, 3 * width : 4 * width]
    keyval = jnp.stack((k_all, v_all))
    pieces = []
    for back in range(WIN - 1, 0, -1):
        pieces.append(passed_along(keyval, "seq", back))
    pieces.append(keyval)
    window = jnp.concatenate(pieces, axis=1)
    q_heads = q_all.reshape(rows, heads, head_dim)
    k_heads = window[0].reshape(WIN * rows, heads, head_dim)
    v_heads = window[1].reshape(WIN * rows, heads, head_dim)
    scores = (
        jnp.einsum("qhd,khd->hqk", q_heads, k_heads, preferred_element_type=jnp.float32) * scale
    )
    weight = jnp.where(allowed[None], jax.nn.silu(scores), 0.0).astype(jnp.bfloat16)
    attn = jnp.einsum("hqk,khd->qhd", weight, v_heads, preferred_element_type=jnp.float32).reshape(
        rows, width
    )
    y_rows = (layer_norm(attn) * u_all.astype(jnp.float32)).astype(jnp.bfloat16)
    x_rows = (
        x_rows.astype(jnp.float32) + jnp.dot(y_rows, w_out[0], preferred_element_type=jnp.float32)
    ).astype(jnp.bfloat16)
    cnormed = layer_norm(c_rows.astype(jnp.float32)).astype(jnp.bfloat16)
    u_c = jax.nn.silu(
        jnp.dot(cnormed, w_in[0][:, 0:width], preferred_element_type=jnp.float32)
    ).astype(jnp.bfloat16)
    q_c = jax.nn.silu(
        jnp.dot(cnormed, w_in[0][:, 2 * width : 3 * width], preferred_element_type=jnp.float32)
    ).astype(jnp.bfloat16)
    all_queries = lax.all_gather(q_c, "seq", axis=0, tiled=True)
    all_users = lax.all_gather(cand_user, "seq", axis=0, tiled=True)
    total_cands = all_queries.shape[0]
    owned = all_users[:, None] == q_seg[None, :]
    cq_heads = all_queries.reshape(total_cands, heads, head_dim)
    own_k = k_all.reshape(rows, heads, head_dim)
    own_v = v_all.reshape(rows, heads, head_dim)
    cscores = (
        jnp.einsum("chd,khd->hck", cq_heads, own_k, preferred_element_type=jnp.float32) * scale
    )
    cweight = jnp.where(owned[None], jax.nn.silu(cscores), 0.0).astype(jnp.bfloat16)
    partial_value = jnp.einsum(
        "hck,khd->chd", cweight, own_v, preferred_element_type=jnp.float32
    ).reshape(total_cands, width)
    cattn = lax.psum_scatter(partial_value, "seq", scatter_dimension=0, tiled=True)
    y_c = (layer_norm(cattn) * u_c.astype(jnp.float32)).astype(jnp.bfloat16)
    c_rows = (
        c_rows.astype(jnp.float32) + jnp.dot(y_c, w_out[0], preferred_element_type=jnp.float32)
    ).astype(jnp.bfloat16)
    return (x_rows, c_rows)


def solution(mesh):
    placed = (
        P(("grp", "seq"), None),
        P(("grp", "seq"), None),
        P("grp"),
        P(("grp", "seq")),
        P(),
        P(),
    )
    return jax.shard_map(
        per_device,
        mesh=mesh,
        in_specs=placed,
        out_specs=(P(("grp", "seq"), None), P(("grp", "seq"), None)),
        check_vma=False,
    )
```

profile of v0, /device:TPU:12, one launch (start us, length us, event | category | flops | bytes accessed | tf_op | source)
XLA Modules:
  0.0 310.7 jit_solution(16720493728466638786)
XLA Ops:
  7.2 0.0 copy-start
  7.2 0.0 reduce-scatter.2.cloned.1.call-start
  7.2 1.3 convert_reduce_fusion
  8.6 1.3 fusion.29
  9.9 6.1 %multiply_convert_fusion = bf16[256,4096]{1,0:T(8,128)(2,1)S(1)} fusion(bf16[256,1024]{1,0:T(8,128)(2,1)} %param.6, f32[256]{0:T(256)S(1)} %add_rsqrt_fusion.1, f32[256]{0:T(256)S(1)} %broadcast_multiply_fusion.1, bf16[1,1024,4096]{2,1,0:T(8,128)(2,1)} %param.10), kind=kOutput, calls=%fused_computation.5 | convolution fusion | flops 2153775104 | bytes 11012096 | tf_op jit(solution)/shard_map/dot_general | solution.py:44
  16.0 0.0 copy-start.1
  16.0 1.4 copy-done.1
  17.4 0.0 copy-start.2
  17.4 0.0 copy-start.3
  17.4 1.4 slice_bitcast_fusion.2
  18.8 1.1 pad_maximum_fusion
  19.9 4.9 %collective-permute-start = (bf16[2,256,1024]{2,1,0:T(8,128)(2,1)}, bf16[2,256,1024]{2,1,0:T(8,128)(2,1)}, u32[]{:S(2)}, u32[]{:S(2)}) collective-permute-start(bf16[2,256,1024]{2,1,0:T(8,128)(2,1)} %pad_maximum_fusion), channel_id=1, source_target_pairs={{0,7},{1,8},{2,9},{3,10},{4,11},{5,12},{6,13},{7,14},{8,15},{16,23... | collective-permute-start | bytes 3145736 | tf_op jit(solution)/shard_map/ppermute | solution.py:14
  24.8 2.3 collective-permute-start.1
  27.0 2.3 collective-permute-start.2
  29.3 1.9 collective-permute-start.3
  31.2 2.1 collective-permute-start.4
  33.3 0.0 copy-done.2
  33.3 0.1 convert_reduce_fusion.1
  33.4 0.2 fusion.60
  33.6 2.0 multiply_convert_fusion.5
  35.7 170.6 %all_gather.7 = bf16[256,1024]{1,0:T(8,128)(2,1)} all-gather(bf16[16,1024]{1,0:T(8,128)(2,1)S(1)} %multiply_convert_fusion.5), channel_id=1, replica_groups=mesh['grp'=2,'seq'=16] {'seq'}, dimensions={0}, use_global_device_ids=true | all-gather | bytes 557056 | tf_op jit(solution)/shard_map/all_gather | solution.py:78
  206.3 0.0 copy-done.3
  206.3 0.2 reduce-window.8
  206.5 0.1 convert_reduce_fusion.3
  206.6 2.1 copy.26
  208.6 0.0 copy-done.5
  208.6 0.6 dynamic-slice
  209.9 0.0 copy-done.4
  209.9 0.2 dynamic-update-slice
  210.1 12.3 %all-reduce = s32[256]{0:T(256)S(1)} all-reduce(s32[256]{0:T(256)S(1)} %dynamic-update-slice), channel_id=1, replica_groups=mesh['grp'=2,'seq'=16] {'seq'}, use_global_device_ids=true, to_apply=%add | all-reduce | flops 256 | bytes 2048
  222.5 0.1 broadcast_compare_fusion
  222.6 3.4 %fusion.17 = f32[8,128,256]{2,1,0:T(8,128)} fusion(bf16[256,8,128]{0,2,1:T(8,128)(2,1)} %bitcast.69, pred[256,256]{1,0:T(8,128)(4,1)S(1)} %broadcast_compare_fusion, bf16[32,8,8,128]{3,2,1,0:T(8,128)(2,1)} %get-tuple-element.4, bf16[256,1024]{1,0:T(8,128)(2,1)} %all_gather.7), kind=kOutput, calls=%fused_computation.21 | convolution fusion | flops 272105472 | bytes 2686976 | tf_op jit(solution)/shard_map/hck,khd->chd/dot_general | solution.py:89
  226.0 2.5 copy.27
  228.5 0.0 reduce-scatter.2.cloned.1.call-update
  228.5 0.1 convert_reduce_fusion.2
  228.6 0.0 collective-permute-done
  228.7 2.8 collective-permute-start.5
  231.4 0.0 collective-permute-done.1
  231.4 1.9 collective-permute-start.6
  233.4 1.7 fusion.14
  235.1 1.3 constant_dynamic-update-slice_fusion.7
  236.4 1.3 constant_dynamic-update-slice_fusion.6
  237.7 0.0 collective-permute-done.2
  237.7 1.3 constant_dynamic-update-slice_fusion.5
  239.0 0.0 collective-permute-done.3
  239.0 1.3 constant_dynamic-update-slice_fusion.4
  240.4 0.0 collective-permute-done.4
  240.4 1.3 constant_dynamic-update-slice_fusion.3
  241.7 17.4 %collective-permute-done.5 = bf16[2,256,1024]{2,1,0:T(8,128)(2,1)S(1)} collective-permute-done((bf16[2,256,1024]{2,1,0:T(8,128)(2,1)}, bf16[2,256,1024]{2,1,0:T(8,128)(2,1)S(1)}, u32[]{:S(2)}, u32[]{:S(2)}) %collective-permute-start.5) | collective-permute-done | bytes 1048608 | tf_op jit(solution)/shard_map/ppermute | solution.py:14
  259.1 0.1 constant_dynamic-update-slice_fusion.2
  259.2 10.7 %collective-permute-done.6 = bf16[2,256,1024]{2,1,0:T(8,128)(2,1)S(1)} collective-permute-done((bf16[2,256,1024]{2,1,0:T(8,128)(2,1)}, bf16[2,256,1024]{2,1,0:T(8,128)(2,1)S(1)}, u32[]{:S(2)}, u32[]{:S(2)}) %collective-permute-start.6) | collective-permute-done | bytes 1048608 | tf_op jit(solution)/shard_map/ppermute | solution.py:14
  269.9 0.1 constant_dynamic-update-slice_fusion.1
  270.0 0.1 constant_dynamic-update-slice_fusion
  270.1 3.0 slice_bitcast_fusion
  273.0 3.1 copy.31
  276.1 6.5 %copy.24 = bf16[1,2048,1024]{1,2,0:T(8,128)(2,1)} copy(bf16[1,2048,1024]{2,1,0:T(8,128)(2,1)} %get-tuple-element.3) | data formatting | bytes 8388608 | tf_op jit(solution)/shard_map/reshape;squeeze | solution.py:59
  282.6 11.7 %fusion.86 = (f32[256]{0:T(256)S(1)}, f32[8,128,256]{2,1,0:T(8,128)S(1)}) fusion(bf16[2048,8,128]{0,2,1:T(8,128)(2,1)} %bitcast.66, pred[256,2048]{1,0:T(8,128)(4,1)} %fusion.14, bf16[2048,8,128]{2,1,0:T(8,128)(2,1)} %bitcast.65, bf16[32,8,8,128]{3,2,1,0:T(8,128)(2,1)} %get-tuple-element.6), kind=kOutput, calls=%fused_computation.99 | convolution fusion | flops 2177105664 | bytes 10486784 | tf_op jit(solution)/shard_map/hqk,khd->qhd/dot_general | solution.py:64
  294.3 1.3 copy.25
  295.6 0.2 fusion.32
  295.8 0.0 copy-done
  295.8 3.1 fusion.18
  298.9 1.0 reduce_sum.98
  299.8 1.0 multiply_reduce_fusion
  300.9 2.9 fusion.26
  (15 shorter events, 0.1 us)
Async XLA Ops:
  7.2 288.6 %copy-start = (bf16[1,1024,1024]{2,1,0:T(8,128)(2,1)S(1)}, bf16[1,1024,1024]{2,1,0:T(8,128)(2,1)}, u32[]{:S(2)}) copy-start(bf16[1,1024,1024]{2,1,0:T(8,128)(2,1)} %param.11) | copy-start | bytes 6291460
  7.2 291.7 %reduce-scatter.2.cloned.1.call-start = ((), (), s32[]{:S(2)}) async-start(), calls=%async_computation.1 | async-start | bytes 1114112 | tf_op jit(solution)/shard_map/reduce_scatter | solution.py:92
  16.0 1.4 copy-start.1
  17.4 15.9 %copy-start.2 = (bf16[16,1024]{1,0:T(8,128)(2,1)S(1)}, bf16[16,1024]{1,0:T(8,128)(2,1)}, u32[]{:S(2)}) copy-start(bf16[16,1024]{1,0:T(8,128)(2,1)} %param.7) | copy-start | bytes 98308
  17.4 188.9 %copy-start.3 = (s32[4]{0:T(128)S(1)}, s32[4]{0:T(128)}, u32[]{:S(2)}) copy-start(s32[4]{0:T(128)} %param.8) | copy-start | bytes 52
  17.4 191.2 %copy-start.5 = (u32[32]{0:T(128)S(1)}, u32[32]{0:T(128)}, u32[]{:S(2)}) copy-start(u32[32]{0:T(128)} %constant.50) | copy-start | bytes 388
  17.4 192.5 %copy-start.4 = (s32[16]{0:T(128)S(1)}, s32[16]{0:T(128)}, u32[]{:S(2)}) copy-start(s32[16]{0:T(128)} %param.9) | copy-start | bytes 196
  19.9 208.8 %collective-permute-start = (bf16[2,256,1024]{2,1,0:T(8,128)(2,1)}, bf16[2,256,1024]{2,1,0:T(8,128)(2,1)}, u32[]{:S(2)}, u32[]{:S(2)}) collective-permute-start(bf16[2,256,1024]{2,1,0:T(8,128)(2,1)} %pad_maximum_fusion), channel_id=1, source_target_pairs={{0,7},{1,8},{2,9},{3,10},{4,11},{5,12},{6,13},{7,14},{8,15},{16,23... | collective-permute-start | bytes 3145736 | tf_op jit(solution)/shard_map/ppermute | solution.py:14
  24.8 206.7 %collective-permute-start.1 = (bf16[2,256,1024]{2,1,0:T(8,128)(2,1)}, bf16[2,256,1024]{2,1,0:T(8,128)(2,1)}, u32[]{:S(2)}, u32[]{:S(2)}) collective-permute-start(bf16[2,256,1024]{2,1,0:T(8,128)(2,1)} %pad_maximum_fusion), channel_id=1, source_target_pairs={{0,6},{1,7},{2,8},{3,9},{4,10},{5,11},{6,12},{7,13},{8,14},{9,15},... | collective-permute-start | bytes 3145736 | tf_op jit(solution)/shard_map/ppermute | solution.py:14
  27.0 210.7 %collective-permute-start.2 = (bf16[2,256,1024]{2,1,0:T(8,128)(2,1)}, bf16[2,256,1024]{2,1,0:T(8,128)(2,1)}, u32[]{:S(2)}, u32[]{:S(2)}) collective-permute-start(bf16[2,256,1024]{2,1,0:T(8,128)(2,1)} %pad_maximum_fusion), channel_id=1, source_target_pairs={{0,5},{1,6},{2,7},{3,8},{4,9},{5,10},{6,11},{7,12},{8,13},{9,14},{... | collective-permute-start | bytes 3145736 | tf_op jit(solution)/shard_map/ppermute | solution.py:14
  29.3 209.7 %collective-permute-start.3 = (bf16[2,256,1024]{2,1,0:T(8,128)(2,1)}, bf16[2,256,1024]{2,1,0:T(8,128)(2,1)}, u32[]{:S(2)}, u32[]{:S(2)}) collective-permute-start(bf16[2,256,1024]{2,1,0:T(8,128)(2,1)} %pad_maximum_fusion), channel_id=1, source_target_pairs={{0,4},{1,5},{2,6},{3,7},{4,8},{5,9},{6,10},{7,11},{8,12},{9,13},{1... | collective-permute-start | bytes 3145736 | tf_op jit(solution)/shard_map/ppermute | solution.py:14
  31.2 209.1 %collective-permute-start.4 = (bf16[2,256,1024]{2,1,0:T(8,128)(2,1)}, bf16[2,256,1024]{2,1,0:T(8,128)(2,1)}, u32[]{:S(2)}, u32[]{:S(2)}) collective-permute-start(bf16[2,256,1024]{2,1,0:T(8,128)(2,1)} %pad_maximum_fusion), channel_id=1, source_target_pairs={{0,3},{1,4},{2,5},{3,6},{4,7},{5,8},{6,9},{7,10},{8,11},{9,12},{10... | collective-permute-start | bytes 3145736 | tf_op jit(solution)/shard_map/ppermute | solution.py:14
  228.7 30.4 %collective-permute-start.5 = (bf16[2,256,1024]{2,1,0:T(8,128)(2,1)}, bf16[2,256,1024]{2,1,0:T(8,128)(2,1)S(1)}, u32[]{:S(2)}, u32[]{:S(2)}) collective-permute-start(bf16[2,256,1024]{2,1,0:T(8,128)(2,1)} %pad_maximum_fusion), channel_id=1, source_target_pairs={{0,2},{1,3},{2,4},{3,5},{4,6},{5,7},{6,8},{7,9},{8,10},{9,11},{10,... | collective-permute-start | bytes 3145736 | tf_op jit(solution)/shard_map/ppermute | solution.py:14
  231.4 38.5 %collective-permute-start.6 = (bf16[2,256,1024]{2,1,0:T(8,128)(2,1)}, bf16[2,256,1024]{2,1,0:T(8,128)(2,1)S(1)}, u32[]{:S(2)}, u32[]{:S(2)}) collective-permute-start(bf16[2,256,1024]{2,1,0:T(8,128)(2,1)} %pad_maximum_fusion), channel_id=1, source_target_pairs={{0,1},{1,2},{2,3},{3,4},{4,5},{5,6},{6,7},{7,8},{8,9},{9,10},{10,1... | collective-permute-start | bytes 3145736 | tf_op jit(solution)/shard_map/ppermute | solution.py:14
Sparse Core Ops, SparseCore 0:
  228.6 59.8 reduce-scatter.1
where the time goes:
time: 312 us; the launch traced here: 311 us
  blocking collectives  183 us (59%)
  matrix products  29.3 us (9%)
  local copies, waits for them, and re-layouts  28.7 us (9%)
  waiting for transfers between devices  28.2 us (9%)
  starting transfers between devices  18.1 us (6%)
  between operations  14.9 us (5%)
  other arithmetic  8.52 us (3%)
    all_gather x1, blocking collectives, per_device(): all_queries = lax.all_gather(q_c, 'seq', axis=0, tiled=True)  171 us
    ppermute x7, waiting for transfers between devices, passed_along(): return lax.ppermute(value, axis, pairs)  28.2 us
    ppermute x7, starting transfers between devices, passed_along(): return lax.ppermute(value, axis, pairs)  18.1 us
    unnamed x25, local copies, waits for them, and re-layouts  16.3 us
    unnamed x1, blocking collectives  12.3 us
    dot_general x1, matrix products, per_device(): jnp.einsum('hqk,khd->qhd', weight, v_heads, preferred_element_type=jnp.fl...  11.7 us
    another operation x1, local copies, waits for them, and re-layouts, per_device(): v_heads = window[1].reshape(WIN * rows, heads, head_dim)  6.5 us
  transfers between devices with their start and end apart: 8, of which 2 were waited for; matrix products, arithmetic and copies ran while one was open for 16% of the time, Pallas kernels for 0%

commit v1 on v0

--- a/solution.py
+++ b/solution.py
@@ -75,7 +75,9 @@
     q_c = jax.nn.silu(
         jnp.dot(cnormed, w_in[0][:, 2 * width : 3 * width], preferred_element_type=jnp.float32)
     ).astype(jnp.bfloat16)
-    all_queries = lax.all_gather(q_c, "seq", axis=0, tiled=True)
+    all_queries = jnp.concatenate(
+        lax.all_to_all(jnp.stack([q_c] * lax.axis_size("seq")), "seq", 0, 0), axis=0
+    )
     all_users = lax.all_gather(cand_user, "seq", axis=0, tiled=True)
     total_cands = all_queries.shape[0]
     owned = all_users[:, None] == q_seg[None, :]

time: 312 us -> 294 us (0.942)
  blocking collectives: 183 us -> 87 us
  starting transfers between devices: 18.1 us -> 85.2 us
  waiting for transfers between devices: 28.2 us -> 33.1 us
  local copies, waits for them, and re-layouts: 28.7 us -> 33 us
    all_gather x1 -> x0, blocking collectives: 171 us -> none  [per_device(): all_queries = lax.all_gather(q_c, 'seq', axis=0, tiled=True)]
    unnamed x1, blocking collectives: 12.3 us -> 87 us
    ppermute x7, starting transfers between devices: 18.1 us -> 76.5 us  [passed_along(): return lax.ppermute(value, axis, pairs)]
    ppermute x7, waiting for transfers between devices: 28.2 us -> 9.41 us  [passed_along(): return lax.ppermute(value, axis, pairs)]
    reduce_scatter x1, waiting for transfers between devices: 0.01 us -> 12.4 us  [per_device(): lax.psum_scatter(partial_value, 'seq', scatter_dimension=0, tiled=True)]
    all_to_all x0 -> x1, waiting for transfers between devices: none -> 11.3 us  [per_device(): lax.all_to_all(jnp.stack([q_c] * lax.axis_size('seq')), 'seq', 0, 0)]
    all_to_all x0 -> x1, starting transfers between devices: none -> 8.64 us  [per_device(): lax.all_to_all(jnp.stack([q_c] * lax.axis_size('seq')), 'seq', 0, 0)]
    unnamed x25 -> x26, local copies, waits for them, and re-layouts: 16.3 us -> 19.7 us
  transfers between devices with their start and end apart: 8 -> 9, of which waited for: 2 -> 3; matrix products, arithmetic and copies ran while one was open for 16% -> 19% of each run, Pallas kernels for 0% -> 0%
where the time goes in v1:
time: 294 us; the launch traced here: 291 us
  blocking collectives  87 us (30%)
  starting transfers between devices  85.2 us (29%)
  waiting for transfers between devices  33.1 us (11%)
  local copies, waits for them, and re-layouts  33 us (11%)
  matrix products  29.3 us (10%)
  between operations  14.9 us (5%)
  other arithmetic  8.54 us (3%)
    unnamed x1, blocking collectives  87 us
    ppermute x7, starting transfers between devices, passed_along(): return lax.ppermute(value, axis, pairs)  76.5 us
    unnamed x26, local copies, waits for them, and re-layouts  19.7 us
    reduce_scatter x1, waiting for transfers between devices, per_device(): lax.psum_scatter(partial_value, 'seq', scatter_dimension=0, tiled=True)  12.4 us
    dot_general x1, matrix products, per_device(): jnp.einsum('hqk,khd->qhd', weight, v_heads, preferred_element_type=jnp.fl...  11.6 us
    all_to_all x1, waiting for transfers between devices, per_device(): lax.all_to_all(jnp.stack([q_c] * lax.axis_size('seq')), 'seq', 0, 0)  11.3 us
    ppermute x7, waiting for transfers between devices, passed_along(): return lax.ppermute(value, axis, pairs)  9.41 us
    all_to_all x1, starting transfers between devices, per_device(): lax.all_to_all(jnp.stack([q_c] * lax.axis_size('seq')), 'seq', 0, 0)  8.64 us
  transfers between devices with their start and end apart: 9, of which 3 were waited for; matrix products, arithmetic and copies ran while one was open for 19% of the time, Pallas kernels for 0%

profile of v1, /device:TPU:12, one launch (start us, length us, event | category | flops | bytes accessed | tf_op | source)
XLA Modules:
  0.0 291.0 jit_solution(16448126225944297806)
XLA Ops:
  7.2 0.0 copy-start
  7.2 1.3 convert_reduce_fusion
  8.5 1.3 fusion.29
  9.9 6.1 %multiply_convert_fusion = bf16[256,4096]{1,0:T(8,128)(2,1)S(1)} fusion(bf16[256,1024]{1,0:T(8,128)(2,1)} %param.6, f32[256]{0:T(256)S(1)} %add_rsqrt_fusion.1, f32[256]{0:T(256)S(1)} %broadcast_multiply_fusion.1, bf16[1,1024,4096]{2,1,0:T(8,128)(2,1)} %param.10), kind=kOutput, calls=%fused_computation.5 | convolution fusion | flops 2153775104 | bytes 11012096 | tf_op jit(solution)/shard_map/dot_general | solution.py:44
  16.0 0.0 copy-start.1
  16.0 0.0 copy-start.2
  16.0 0.0 copy-start.3
  16.0 1.7 slice_bitcast_fusion.2
  17.8 1.1 pad_maximum_fusion
  18.8 4.9 %collective-permute-start = (bf16[2,256,1024]{2,1,0:T(8,128)(2,1)}, bf16[2,256,1024]{2,1,0:T(8,128)(2,1)}, u32[]{:S(2)}, u32[]{:S(2)}) collective-permute-start(bf16[2,256,1024]{2,1,0:T(8,128)(2,1)} %pad_maximum_fusion), channel_id=1, source_target_pairs={{0,7},{1,8},{2,9},{3,10},{4,11},{5,12},{6,13},{7,14},{8,15},{16,23... | collective-permute-start | bytes 3145736 | tf_op jit(solution)/shard_map/ppermute | solution.py:14
  23.7 2.3 collective-permute-start.1
  26.0 2.3 collective-permute-start.2
  28.3 1.9 collective-permute-start.3
  30.2 2.1 collective-permute-start.4
  32.2 0.0 copy-done.2
  32.3 0.1 convert_reduce_fusion.1
  32.4 0.2 fusion.58
  32.6 2.0 multiply_convert_fusion.5
  34.6 0.0 copy-done.1
  34.6 0.9 stack.11
  35.5 8.6 %all-to-all-start = ((bf16[16,16,1024]{2,1,0:T(8,128)(2,1)}), bf16[16,16,1024]{2,1,0:T(8,128)(2,1)}, u32[]{:S(2)}, u32[]{:S(2)}) async-start(bf16[16,16,1024]{2,1,0:T(8,128)(2,1)} %stack.11), calls=%async_computation | async-start | bytes 1048576 | tf_op jit(solution)/shard_map/all_to_all | solution.py:79
  44.2 0.0 reduce-scatter.2.cloned.1.call-start
  44.3 0.2 reduce-window.8
  44.4 0.1 convert_reduce_fusion.3
  44.5 0.1 convert_reduce_fusion.2
  44.6 1.7 fusion.14
  46.3 0.6 dynamic-slice
  47.6 0.2 dynamic-update-slice
  47.8 87.0 %all-reduce = s32[256]{0:T(256)S(1)} all-reduce(s32[256]{0:T(256)S(1)} %dynamic-update-slice), channel_id=1, replica_groups=mesh['grp'=2,'seq'=16] {'seq'}, use_global_device_ids=true, to_apply=%add | all-reduce | flops 256 | bytes 2048
  134.9 0.1 broadcast_compare_fusion
  135.0 2.1 copy.33
  137.0 11.3 %all-to-all-done = bf16[16,16,1024]{2,1,0:T(8,128)(2,1)} async-done(((bf16[16,16,1024]{2,1,0:T(8,128)(2,1)}), bf16[16,16,1024]{2,1,0:T(8,128)(2,1)}, u32[]{:S(2)}, u32[]{:S(2)}) %all-to-all-start) | async-done | bytes 524320 | tf_op jit(solution)/shard_map/all_to_all | solution.py:79
  148.3 2.0 copy.38
  150.3 0.0 collective-permute-done
  150.3 61.2 %collective-permute-start.5 = (bf16[2,256,1024]{2,1,0:T(8,128)(2,1)}, bf16[2,256,1024]{2,1,0:T(8,128)(2,1)}, u32[]{:S(2)}, u32[]{:S(2)}) collective-permute-start(bf16[2,256,1024]{2,1,0:T(8,128)(2,1)} %pad_maximum_fusion), channel_id=1, source_target_pairs={{0,2},{1,3},{2,4},{3,5},{4,6},{5,7},{6,8},{7,9},{8,10},{9,11},{10,... | collective-permute-start | bytes 3145736 | tf_op jit(solution)/shard_map/ppermute | solution.py:14
  211.4 0.0 collective-permute-done.1
  211.5 1.9 collective-permute-start.6
  213.4 3.4 %fusion.17 = f32[8,128,256]{2,1,0:T(8,128)} fusion(bf16[256,8,128]{0,2,1:T(8,128)(2,1)} %bitcast.63, pred[256,256]{1,0:T(8,128)(4,1)S(1)} %broadcast_compare_fusion, bf16[32,8,8,128]{3,2,1,0:T(8,128)(2,1)} %get-tuple-element.4, bf16[256,8,128]{2,1,0:T(8,128)(2,1)} %bitcast.64), kind=kOutput, calls=%fused_computation.21 | convolution fusion | flops 272105472 | bytes 2686976 | tf_op jit(solution)/shard_map/hck,khd->chd/dot_general | solution.py:91
  216.8 2.5 copy.34
  219.4 0.0 reduce-scatter.2.cloned.1.call-update
  219.4 1.3 constant_dynamic-update-slice_fusion.7
  220.7 1.3 constant_dynamic-update-slice_fusion.6
  222.0 0.0 collective-permute-done.2
  222.0 1.3 constant_dynamic-update-slice_fusion.5
  223.3 0.0 collective-permute-done.3
  223.3 1.3 constant_dynamic-update-slice_fusion.4
  224.6 0.0 collective-permute-done.4
  224.6 1.3 constant_dynamic-update-slice_fusion.3
  225.9 9.4 %collective-permute-done.5 = bf16[2,256,1024]{2,1,0:T(8,128)(2,1)} collective-permute-done((bf16[2,256,1024]{2,1,0:T(8,128)(2,1)}, bf16[2,256,1024]{2,1,0:T(8,128)(2,1)}, u32[]{:S(2)}, u32[]{:S(2)}) %collective-permute-start.5) | collective-permute-done | bytes 1048608 | tf_op jit(solution)/shard_map/ppermute | solution.py:14
  235.3 1.3 constant_dynamic-update-slice_fusion.2
  236.6 0.0 collective-permute-done.6
  236.6 1.3 constant_dynamic-update-slice_fusion.1
  237.9 0.1 constant_dynamic-update-slice_fusion
  238.0 3.0 %slice_bitcast_fusion = (bf16[256,8,8,128]{3,1,2,0:T(8,128)(2,1)S(1)}, bf16[1,2048,1024]{2,1,0:T(8,128)(2,1)}) fusion(bf16[2,2048,1024]{2,1,0:T(8,128)(2,1)S(1)} %constant_dynamic-update-slice_fusion), kind=kLoop, calls=%fused_computation.3 | loop fusion | bytes 16777216
  241.0 3.1 %copy.37 = bf16[256,8,8,128]{3,2,1,0:T(8,128)(2,1)} copy(bf16[256,8,8,128]{3,1,2,0:T(8,128)(2,1)S(1)} %get-tuple-element.2) | data formatting | bytes 8388608
  244.0 6.6 %copy.31 = bf16[1,2048,1024]{1,2,0:T(8,128)(2,1)} copy(bf16[1,2048,1024]{2,1,0:T(8,128)(2,1)} %get-tuple-element.3) | data formatting | bytes 8388608 | tf_op jit(solution)/shard_map/reshape;squeeze | solution.py:59
  250.6 11.6 %fusion.84 = (f32[256]{0:T(256)S(1)}, f32[8,128,256]{2,1,0:T(8,128)S(1)}) fusion(bf16[2048,8,128]{0,2,1:T(8,128)(2,1)} %bitcast.60, pred[256,2048]{1,0:T(8,128)(4,1)} %fusion.14, bf16[2048,8,128]{2,1,0:T(8,128)(2,1)} %bitcast.59, bf16[32,8,8,128]{3,2,1,0:T(8,128)(2,1)} %get-tuple-element.6), kind=kOutput, calls=%fused_computation.98 | convolution fusion | flops 2177105664 | bytes 10486784 | tf_op jit(solution)/shard_map/hqk,khd->qhd/dot_general | solution.py:64
  262.2 1.3 copy.32
  263.6 0.2 fusion.32
  263.7 3.1 %fusion.18 = bf16[256,1024]{1,0:T(8,128)(2,1)} fusion(bf16[1,1024,1024]{2,1,0:T(8,128)(2,1)S(1)} %copy-done, bf16[256,1024]{1,0:T(8,128)(2,1)} %param.6, f32[256,1024]{1,0:T(8,128)} %copy.32, bf16[256,4096]{1,0:T(8,128)(2,1)} %copy-done.1, f32[256]{0:T(256)S(1)} %add_rsqrt_fusion, f32[256]{0:T(256)S(1)} %broadcast_multiply_fusion), kind=kOutput, calls=%fused_computation.22 | convolution fusion | flops 538968064 | bytes 4720640 | tf_op jit(solution)/shard_map/dot_general | solution.py:69
  266.8 12.4 %reduce-scatter.2.cloned.1.call-done = f32[16,1024]{1,0:T(8,128)} async-done(((f32[256,1024]{1,0:T(8,128)}), f32[16,1024]{1,0:T(8,128)}) %reduce-scatter.2.cloned.1.call-update) | async-done | bytes 65552 | tf_op jit(solution)/shard_map/reduce_scatter | solution.py:94
  279.2 1.0 reduce_sum.98
  280.2 1.0 multiply_reduce_fusion
  281.2 2.9 %fusion.26 = bf16[16,1024]{1,0:T(8,128)(2,1)} fusion(bf16[1,1024,1024]{2,1,0:T(8,128)(2,1)S(1)} %copy-done, bf16[16,1024]{1,0:T(8,128)(2,1)S(1)} %copy-done.2, bf16[1024,4096]{1,0:T(8,128)(2,1)} %bitcast.66, f32[16,1024]{1,0:T(8,128)} %reduce-scatter.2.cloned.1.call-done, f32[16]{0:T(128)S(1)} %add_rsqrt_fusion.2, f32[16]{0:T(128)S(1)} %broadcast_multiply_fusion.2, ...), kind=kOutput, calls=%fused_computation.26 | convolution fusion | flops 67387392 | bytes 4360192 | tf_op jit(solution)/shard_map/dot_general | solution.py:97
  (18 shorter events, 0.1 us)
Async XLA Ops:
  7.2 256.6 %copy-start = (bf16[1,1024,1024]{2,1,0:T(8,128)(2,1)S(1)}, bf16[1,1024,1024]{2,1,0:T(8,128)(2,1)}, u32[]{:S(2)}) copy-start(bf16[1,1024,1024]{2,1,0:T(8,128)(2,1)} %param.11) | copy-start | bytes 6291460
  16.0 18.6 %copy-start.1 = (bf16[256,4096]{1,0:T(8,128)(2,1)}, bf16[256,4096]{1,0:T(8,128)(2,1)S(1)}, u32[]{:S(2)}) copy-start(bf16[256,4096]{1,0:T(8,128)(2,1)S(1)} %multiply_convert_fusion) | copy-start | bytes 6291460
  16.0 16.2 %copy-start.2 = (bf16[16,1024]{1,0:T(8,128)(2,1)S(1)}, bf16[16,1024]{1,0:T(8,128)(2,1)}, u32[]{:S(2)}) copy-start(bf16[16,1024]{1,0:T(8,128)(2,1)} %param.7) | copy-start | bytes 98308
  16.0 28.2 %copy-start.3 = (s32[4]{0:T(128)S(1)}, s32[4]{0:T(128)}, u32[]{:S(2)}) copy-start(s32[4]{0:T(128)} %param.8) | copy-start | bytes 52
  17.8 28.6 %copy-start.5 = (u32[32]{0:T(128)S(1)}, u32[32]{0:T(128)}, u32[]{:S(2)}) copy-start(u32[32]{0:T(128)} %constant.50) | copy-start | bytes 388
  17.8 29.8 %copy-start.4 = (s32[16]{0:T(128)S(1)}, s32[16]{0:T(128)}, u32[]{:S(2)}) copy-start(s32[16]{0:T(128)} %param.9) | copy-start | bytes 196
  18.8 131.4 %collective-permute-start = (bf16[2,256,1024]{2,1,0:T(8,128)(2,1)}, bf16[2,256,1024]{2,1,0:T(8,128)(2,1)}, u32[]{:S(2)}, u32[]{:S(2)}) collective-permute-start(bf16[2,256,1024]{2,1,0:T(8,128)(2,1)} %pad_maximum_fusion), channel_id=1, source_target_pairs={{0,7},{1,8},{2,9},{3,10},{4,11},{5,12},{6,13},{7,14},{8,15},{16,23... | collective-permute-start | bytes 3145736 | tf_op jit(solution)/shard_map/ppermute | solution.py:14
  23.7 187.7 %collective-permute-start.1 = (bf16[2,256,1024]{2,1,0:T(8,128)(2,1)}, bf16[2,256,1024]{2,1,0:T(8,128)(2,1)}, u32[]{:S(2)}, u32[]{:S(2)}) collective-permute-start(bf16[2,256,1024]{2,1,0:T(8,128)(2,1)} %pad_maximum_fusion), channel_id=1, source_target_pairs={{0,6},{1,7},{2,8},{3,9},{4,10},{5,11},{6,12},{7,13},{8,14},{9,15},... | collective-permute-start | bytes 3145736 | tf_op jit(solution)/shard_map/ppermute | solution.py:14
  26.0 196.0 %collective-permute-start.2 = (bf16[2,256,1024]{2,1,0:T(8,128)(2,1)}, bf16[2,256,1024]{2,1,0:T(8,128)(2,1)}, u32[]{:S(2)}, u32[]{:S(2)}) collective-permute-start(bf16[2,256,1024]{2,1,0:T(8,128)(2,1)} %pad_maximum_fusion), channel_id=1, source_target_pairs={{0,5},{1,6},{2,7},{3,8},{4,9},{5,10},{6,11},{7,12},{8,13},{9,14},{... | collective-permute-start | bytes 3145736 | tf_op jit(solution)/shard_map/ppermute | solution.py:14
  28.3 195.0 %collective-permute-start.3 = (bf16[2,256,1024]{2,1,0:T(8,128)(2,1)}, bf16[2,256,1024]{2,1,0:T(8,128)(2,1)}, u32[]{:S(2)}, u32[]{:S(2)}) collective-permute-start(bf16[2,256,1024]{2,1,0:T(8,128)(2,1)} %pad_maximum_fusion), channel_id=1, source_target_pairs={{0,4},{1,5},{2,6},{3,7},{4,8},{5,9},{6,10},{7,11},{8,12},{9,13},{1... | collective-permute-start | bytes 3145736 | tf_op jit(solution)/shard_map/ppermute | solution.py:14
  30.2 194.4 %collective-permute-start.4 = (bf16[2,256,1024]{2,1,0:T(8,128)(2,1)}, bf16[2,256,1024]{2,1,0:T(8,128)(2,1)}, u32[]{:S(2)}, u32[]{:S(2)}) collective-permute-start(bf16[2,256,1024]{2,1,0:T(8,128)(2,1)} %pad_maximum_fusion), channel_id=1, source_target_pairs={{0,3},{1,4},{2,5},{3,6},{4,7},{5,8},{6,9},{7,10},{8,11},{9,12},{10... | collective-permute-start | bytes 3145736 | tf_op jit(solution)/shard_map/ppermute | solution.py:14
  35.5 112.8 %all-to-all-start = ((bf16[16,16,1024]{2,1,0:T(8,128)(2,1)}), bf16[16,16,1024]{2,1,0:T(8,128)(2,1)}, u32[]{:S(2)}, u32[]{:S(2)}) async-start(bf16[16,16,1024]{2,1,0:T(8,128)(2,1)} %stack.11), calls=%async_computation | async-start | bytes 1048576 | tf_op jit(solution)/shard_map/all_to_all | solution.py:79
  44.2 235.0 %reduce-scatter.2.cloned.1.call-start = ((), (), s32[]{:S(2)}) async-start(), calls=%async_computation.2 | async-start | bytes 1114112 | tf_op jit(solution)/shard_map/reduce_scatter | solution.py:94
  150.3 85.0 %collective-permute-start.5 = (bf16[2,256,1024]{2,1,0:T(8,128)(2,1)}, bf16[2,256,1024]{2,1,0:T(8,128)(2,1)}, u32[]{:S(2)}, u32[]{:S(2)}) collective-permute-start(bf16[2,256,1024]{2,1,0:T(8,128)(2,1)} %pad_maximum_fusion), channel_id=1, source_target_pairs={{0,2},{1,3},{2,4},{3,5},{4,6},{5,7},{6,8},{7,9},{8,10},{9,11},{10,... | collective-permute-start | bytes 3145736 | tf_op jit(solution)/shard_map/ppermute | solution.py:14
  211.5 25.1 %collective-permute-start.6 = (bf16[2,256,1024]{2,1,0:T(8,128)(2,1)}, bf16[2,256,1024]{2,1,0:T(8,128)(2,1)}, u32[]{:S(2)}, u32[]{:S(2)}) collective-permute-start(bf16[2,256,1024]{2,1,0:T(8,128)(2,1)} %pad_maximum_fusion), channel_id=1, source_target_pairs={{0,1},{1,2},{2,3},{3,4},{4,5},{5,6},{6,7},{7,8},{8,9},{9,10},{10,1... | collective-permute-start | bytes 3145736 | tf_op jit(solution)/shard_map/ppermute | solution.py:14
Sparse Core Ops, SparseCore 0:
  219.5 59.6 reduce-scatter.1
